TPU v7x, 32 devices: a whole 2x2x4 slice. The times are simulated.
32 devices in a mesh: dp: 16 (over z, y, core), mlp: 2 (over x).
Axes of the slice: x: 2, y: 2, z: 4, core: 2. Of those that a mesh axis runs over, the one named last changes fastest.
Arguments:
- block_input: bfloat16 [16, 2, 160, 1024], P('dp', 'mlp'), may hold values from -6 to 6
- span_offset: int32 [16, 2], replicated, may hold values from 0 to 15, as said below
- ln_gain: float32 [1024], replicated, may hold values from 0.5 to 1.5
- ln_bias: float32 [1024], replicated, may hold values from -3 to 3
- w_qkv: bfloat16 [1024, 3072], replicated, may hold values from -0.25 to 0.25
- b_qkv: float32 [3072], replicated, may hold values from -3 to 3
- w_out: bfloat16 [1024, 1024], replicated, may hold values from -1 to 1
- b_out: float32 [1024], replicated, may hold values from -3 to 3
- w_up: bfloat16 [1024, 4096], P(None, 'mlp'), may hold values from -0.1875 to 0.1875
- b_up: float32 [4096], P('mlp'), may hold values from -3 to 3
- w_down: bfloat16 [4096, 1024], P('mlp'), may hold values from -0.09375 to 0.09375
- b_down: float32 [1024], replicated, may hold values from -3 to 3
- cotangent: bfloat16 [16, 2, 160, 1024], P('dp', 'mlp'), may hold values from -6 to 6
Outputs:
- output: bfloat16 [16, 2, 160, 1024], P('dp', 'mlp')
- grad_input: float32 [16, 2, 160, 1024], P('dp', 'mlp')
- grad_ln_gain: float32 [1024], P('mlp')
- grad_ln_bias: float32 [1024], P('mlp')
- grad_w_qkv: float32 [1024, 3072], P(None, 'mlp')
- grad_b_qkv: float32 [3072], P('mlp')
- grad_w_out: float32 [1024, 1024], P(None, 'mlp')
- grad_b_out: float32 [1024], P('mlp')
- grad_w_up: float32 [1024, 4096], P(None, 'mlp')
- grad_b_up: float32 [4096], P('mlp')
- grad_w_down: float32 [4096, 1024], P('mlp')
- grad_b_down: float32 [1024], P('mlp')
Inputs may be any that keep to these rules, and one draw needn't show every extreme that they name: For every sequence s, span_offset[:, s] is a permutation of 0 to 15.
All inputs are finite; a program needn't handle non-finite values.
Results may differ from a plain program's by a relative error of at most 0.02.
Values may be sent and summed in bfloat16 or wider, within the bound.
A program may use at most 256 MiB of HBM per device.

v0:
```python
import math
import jax
import jax.numpy as jnp
from jax import lax
from jax.sharding import PartitionSpec as P

HEADS = 16
HEAD_DIM = 64
ROT = 16
EPSILON = 1e-05
ROPE_BASE = 10000.0
SQRT_HALF = 1.0 / math.sqrt(2.0)
INV_ROOT_TWO_PI = 1.0 / math.sqrt(2.0 * math.pi)


def rotate(values, positions, sign_factor):
    half_rot = ROT // 2
    frequency = ROPE_BASE ** (-(jnp.arange(half_rot, dtype=jnp.float32) * 2.0 / ROT))
    angles = positions.astype(jnp.float32)[:, None] * frequency[None, :]
    cosine = jnp.cos(angles)[:, None, :]
    sine_part = sign_factor * jnp.sin(angles)[:, None, :]
    first_half = values[..., :half_rot]
    second_half = values[..., half_rot:ROT]
    return jnp.concatenate(
        [
            first_half * cosine - second_half * sine_part,
            second_half * cosine + first_half * sine_part,
            values[..., ROT:],
        ],
        axis=-1,
    )


def gelu_exact(values):
    return 0.5 * values * (1.0 + lax.erf(values * SQRT_HALF))


def gelu_slope(values):
    return (
        0.5 * (1.0 + lax.erf(values * SQRT_HALF))
        + values * jnp.exp(-0.5 * values * values) * INV_ROOT_TWO_PI
    )


def piece_count(total_rows):
    count_blocks = max(1, total_rows // 1024)
    while total_rows % count_blocks:
        count_blocks += 1
    return count_blocks


def row_positions(offsets, count_rows, tok_count):
    index_all = jnp.arange(count_rows, dtype=jnp.int32)
    span_of = index_all // tok_count
    within = index_all - span_of * tok_count
    matches = span_of[:, None] == jnp.arange(offsets.shape[0], dtype=jnp.int32)[None, :]
    offset_of = jnp.sum(jnp.where(matches, offsets[None, :], 0), axis=1)
    return offset_of * tok_count + within


def contract_rows(left_mat, right_mat):
    return lax.dot_general(
        left_mat, right_mat, (((0,), (0,)), ((), ())), preferred_element_type=jnp.float32
    )


def contract_cols(left_mat, right_mat):
    return lax.dot_general(
        left_mat, right_mat, (((1,), (1,)), ((), ())), preferred_element_type=jnp.float32
    )


def local(
    block_input,
    span_offset,
    ln_gain,
    ln_bias,
    w_qkv,
    b_qkv,
    w_out,
    b_out,
    w_up,
    b_up,
    w_down,
    b_down,
    cotangent,
):
    tok_count = block_input.shape[2]
    model_width = block_input.shape[3]
    scale_dot = 1.0 / math.sqrt(HEAD_DIM)
    span_here = lax.axis_index("dp")
    seq_here = lax.axis_index("mlp")
    offsets = lax.dynamic_index_in_dim(span_offset, seq_here, axis=1, keepdims=False)
    offset_here = lax.dynamic_index_in_dim(offsets, span_here, axis=0, keepdims=False)
    positions = offset_here * tok_count + jnp.arange(tok_count, dtype=jnp.int32)
    row_data = block_input[0, 0].astype(jnp.float32)
    centre = jnp.mean(row_data, axis=-1, keepdims=True)
    centred = row_data - centre
    spread = jnp.mean(centred * centred, axis=-1, keepdims=True)
    inv_scale = lax.rsqrt(spread + EPSILON)
    unit_rows = centred * inv_scale
    normed = (unit_rows * ln_gain + ln_bias).astype(jnp.bfloat16)
    project = jnp.dot(normed, w_qkv, preferred_element_type=jnp.float32) + b_qkv
    queries = rotate(
        project[:, :model_width].reshape(tok_count, HEADS, HEAD_DIM), positions, 1.0
    ).astype(jnp.bfloat16)
    keys_here = rotate(
        project[:, model_width : 2 * model_width].reshape(tok_count, HEADS, HEAD_DIM),
        positions,
        1.0,
    ).astype(jnp.bfloat16)
    values_here = (
        project[:, 2 * model_width :].reshape(tok_count, HEADS, HEAD_DIM).astype(jnp.bfloat16)
    )
    keys_flat = keys_here.reshape(tok_count, model_width)
    values_flat = values_here.reshape(tok_count, model_width)
    start_state = (
        jnp.zeros((tok_count, HEADS, HEAD_DIM), jnp.float32),
        jnp.zeros((HEADS, tok_count), jnp.float32),
    )
    keys_piece = lax.all_gather(keys_flat, "dp", axis=0, tiled=True)
    values_piece = lax.all_gather(values_flat, "dp", axis=0, tiled=True)
    piece_rows = keys_piece.shape[0]
    blocks = piece_count(piece_rows)
    sub_rows = piece_rows // blocks
    key_pos = row_positions(offsets, piece_rows, tok_count)

    def attend_one_block(state_now, packed):
        keys_blk, values_blk, pos_blk = packed
        key_heads = keys_blk.reshape(sub_rows, HEADS, HEAD_DIM)
        value_heads = values_blk.reshape(sub_rows, HEADS, HEAD_DIM)
        scores = (
            jnp.einsum("qhd,khd->hqk", queries, key_heads, preferred_element_type=jnp.float32)
            * scale_dot
        )
        allowed = pos_blk[None, :] <= positions[:, None]
        weights_exp = jnp.where(allowed[None], jnp.exp(scores), 0.0)
        mixed_sum, totals = state_now
        mixed_sum = mixed_sum + jnp.einsum(
            "hqk,khd->qhd",
            weights_exp.astype(jnp.bfloat16),
            value_heads,
            preferred_element_type=jnp.float32,
        )
        return ((mixed_sum, totals + jnp.sum(weights_exp, axis=-1)), None)

    state_now, _unused = lax.scan(
        attend_one_block,
        start_state,
        (
            keys_piece.reshape(blocks, sub_rows, model_width),
            values_piece.reshape(blocks, sub_rows, model_width),
            key_pos.reshape(blocks, sub_rows),
        ),
    )
    mixed_sum, totals = state_now
    attended = mixed_sum / totals.T[:, :, None]
    attended_low = attended.reshape(tok_count, model_width).astype(jnp.bfloat16)
    attn_branch = jnp.dot(attended_low, w_out, preferred_element_type=jnp.float32) + b_out
    normed_all = lax.all_gather(normed, "mlp", axis=0, tiled=True)
    up_proj = jnp.dot(normed_all, w_up, preferred_element_type=jnp.float32) + b_up
    activated = gelu_exact(up_proj).astype(jnp.bfloat16)
    mlp_branch = (
        lax.psum_scatter(
            jnp.dot(activated, w_down, preferred_element_type=jnp.float32).astype(jnp.bfloat16),
            "mlp",
            scatter_dimension=0,
            tiled=True,
        ).astype(jnp.float32)
        + b_down
    )
    output = (row_data + attn_branch + mlp_branch).astype(jnp.bfloat16)
    grad_out = cotangent[0, 0]
    grad_w_out = contract_rows(attended_low, grad_out)
    grad_bias_out = jnp.sum(grad_out.astype(jnp.float32), axis=0)
    grad_all = lax.all_gather(grad_out, "mlp", axis=0, tiled=True)
    grad_w_down = contract_rows(activated, grad_all)
    grad_act = contract_cols(grad_all, w_down)
    grad_up = (grad_act * gelu_slope(up_proj)).astype(jnp.bfloat16)
    grad_w_up = contract_rows(normed_all, grad_up)
    grad_b_up = jnp.sum(grad_up.astype(jnp.float32), axis=0)
    grad_norm_mlp = lax.psum_scatter(
        contract_cols(grad_up, w_up).astype(jnp.bfloat16), "mlp", scatter_dimension=0, tiled=True
    ).astype(jnp.float32)
    grad_att = contract_cols(grad_out, w_out).reshape(tok_count, HEADS, HEAD_DIM)
    grad_mixed = (grad_att / totals.T[:, :, None]).astype(jnp.bfloat16)
    grad_totals = ((-jnp.sum(grad_att * attended, axis=-1)).T / totals).astype(jnp.bfloat16)
    grad_totals_wide = grad_totals.astype(jnp.float32)[:, :, None]
    zero_heads = jnp.zeros((tok_count, HEADS, HEAD_DIM), jnp.float32)
    grad_query_sum = zero_heads
    keys_piece = lax.all_gather(keys_flat, "dp", axis=0, tiled=True)
    values_piece = lax.all_gather(values_flat, "dp", axis=0, tiled=True)
    piece_rows = keys_piece.shape[0]
    blocks = piece_count(piece_rows)
    back_sub_rows = piece_rows // blocks
    key_pos = row_positions(offsets, piece_rows, tok_count)

    def back_one_block(running_sum, packed):
        keys_blk, values_blk, pos_blk = packed
        key_heads = keys_blk.reshape(back_sub_rows, HEADS, HEAD_DIM)
        value_heads = values_blk.reshape(back_sub_rows, HEADS, HEAD_DIM)
        scores = (
            jnp.einsum("qhd,khd->hqk", queries, key_heads, preferred_element_type=jnp.float32)
            * scale_dot
        )
        allowed = pos_blk[None, :] <= positions[:, None]
        weights_exp = jnp.where(allowed[None], jnp.exp(scores), 0.0)
        grad_exp = jnp.einsum(
            "qhd,khd->hqk", grad_mixed, value_heads, preferred_element_type=jnp.float32
        )
        grad_scores = (weights_exp * (grad_exp + grad_totals_wide)).astype(jnp.bfloat16)
        running_sum = running_sum + scale_dot * jnp.einsum(
            "hqk,khd->qhd", grad_scores, key_heads, preferred_element_type=jnp.float32
        )
        grad_key_blk = scale_dot * jnp.einsum(
            "hqk,qhd->khd", grad_scores, queries, preferred_element_type=jnp.float32
        )
        grad_value_blk = jnp.einsum(
            "hqk,qhd->khd",
            weights_exp.astype(jnp.bfloat16),
            grad_mixed,
            preferred_element_type=jnp.float32,
        )
        joined = jnp.concatenate(
            [
                grad_key_blk.reshape(back_sub_rows, model_width),
                grad_value_blk.reshape(back_sub_rows, model_width),
            ],
            axis=1,
        )
        return (running_sum, joined)

    grad_query_sum, stacked = lax.scan(
        back_one_block,
        grad_query_sum,
        (
            keys_piece.reshape(blocks, back_sub_rows, model_width),
            values_piece.reshape(blocks, back_sub_rows, model_width),
            key_pos.reshape(blocks, back_sub_rows),
        ),
    )
    grad_kv_sum = stacked.reshape(piece_rows, 2 * model_width)
    grad_kv = lax.psum_scatter(
        grad_kv_sum.astype(jnp.bfloat16), "dp", scatter_dimension=0, tiled=True
    ).astype(jnp.float32)
    grad_keys = grad_kv[:, :model_width].reshape(tok_count, HEADS, HEAD_DIM)
    grad_values = grad_kv[:, model_width:].reshape(tok_count, HEADS, HEAD_DIM)
    grad_query_pre = rotate(grad_query_sum, positions, -1.0).reshape(tok_count, model_width)
    grad_key_pre = rotate(grad_keys, positions, -1.0).reshape(tok_count, model_width)
    grad_project = jnp.concatenate(
        [grad_query_pre, grad_key_pre, grad_values.reshape(tok_count, model_width)], axis=1
    ).astype(jnp.bfloat16)
    grad_w_qkv = contract_rows(normed, grad_project)
    grad_b_qkv = jnp.sum(grad_project.astype(jnp.float32), axis=0)
    grad_normed = contract_cols(grad_project, w_qkv) + grad_norm_mlp
    grad_ln_gain = jnp.sum(grad_normed * unit_rows, axis=0)
    grad_ln_bias = jnp.sum(grad_normed, axis=0)
    grad_unit = grad_normed * ln_gain
    grad_rows = inv_scale * (
        grad_unit
        - jnp.mean(grad_unit, axis=-1, keepdims=True)
        - unit_rows * jnp.mean(grad_unit * unit_rows, axis=-1, keepdims=True)
    )
    grad_input = (grad_out.astype(jnp.float32) + grad_rows).reshape(1, 1, tok_count, model_width)
    part_qkv, part_out, part_bqkv, part_bias, part_gain, part_shift = (
        lax.psum_scatter(
            grad_w_qkv.astype(jnp.bfloat16), "mlp", scatter_dimension=1, tiled=True
        ).astype(jnp.float32),
        lax.psum_scatter(
            grad_w_out.astype(jnp.bfloat16), "mlp", scatter_dimension=1, tiled=True
        ).astype(jnp.float32),
        lax.psum_scatter(
            grad_b_qkv.astype(jnp.bfloat16), "mlp", scatter_dimension=0, tiled=True
        ).astype(jnp.float32),
        lax.psum_scatter(
            grad_bias_out.astype(jnp.bfloat16), "mlp", scatter_dimension=0, tiled=True
        ).astype(jnp.float32),
        lax.psum_scatter(
            grad_ln_gain.astype(jnp.bfloat16), "mlp", scatter_dimension=0, tiled=True
        ).astype(jnp.float32),
        lax.psum_scatter(
            grad_ln_bias.astype(jnp.bfloat16), "mlp", scatter_dimension=0, tiled=True
        ).astype(jnp.float32),
    )
    summed = (
        lax.psum(part_qkv.astype(jnp.bfloat16), "dp").astype(jnp.float32),
        lax.psum(part_out.astype(jnp.bfloat16), "dp").astype(jnp.float32),
        lax.psum(part_bqkv.astype(jnp.bfloat16), "dp").astype(jnp.float32),
        lax.psum(part_bias.astype(jnp.bfloat16), "dp").astype(jnp.float32),
        lax.psum(part_gain.astype(jnp.bfloat16), "dp").astype(jnp.float32),
        lax.psum(part_shift.astype(jnp.bfloat16), "dp").astype(jnp.float32),
        lax.psum(grad_w_up.astype(jnp.bfloat16), "dp").astype(jnp.float32),
        lax.psum(grad_b_up.astype(jnp.bfloat16), "dp").astype(jnp.float32),
        lax.psum(grad_w_down.astype(jnp.bfloat16), "dp").astype(jnp.float32),
    )
    return (
        output.reshape(1, 1, tok_count, model_width),
        grad_input,
        summed[4],
        summed[5],
        summed[0],
        summed[2],
        summed[1],
        summed[3],
        summed[6],
        summed[7],
        summed[8],
        summed[3],
    )


def solution(mesh):
    return jax.shard_map(
        local,
        mesh=mesh,
        in_specs=(
            P("dp", "mlp", None, None),
            P(),
            P(),
            P(),
            P(),
            P(),
            P(),
            P(),
            P(None, "mlp"),
            P("mlp"),
            P("mlp", None),
            P(),
            P("dp", "mlp", None, None),
        ),
        out_specs=(
            P("dp", "mlp", None, None),
            P("dp", "mlp", None, None),
            P("mlp"),
            P("mlp"),
            P(None, "mlp"),
            P("mlp"),
            P(None, "mlp"),
            P("mlp"),
            P(None, "mlp"),
            P("mlp"),
            P("mlp", None),
            P("mlp"),
        ),
        check_vma=False,
    )
```

profile of v0, /device:TPU:0, one launch (start us, length us, event | category | flops | bytes accessed | tf_op | source)
XLA Modules:
  0.0 848.6 jit_solution(7495591158141131622)
XLA Ops:
  15.1 4.1 convolution_add_fusion
  25.3 2.8 subtract_convert_fusion.1
  29.5 2.3 convert_element_type.149
  31.9 1.9 slice.115
  35.4 2.1 pad_maximum_fusion.2
  38.3 52.1 %all-gather.6.cloned.1.call-done = bf16[2560,1024]{1,0:T(8,128)(2,1)} async-done(((bf16[160,1024]{1,0:T(8,128)(2,1)}), bf16[2560,1024]{1,0:T(8,128)(2,1)}) %all-gather.6.cloned.1.call-update) | async-done | bytes 5242896 | tf_op jit(solution)/shard_map/all_gather | solution.py:121
  90.4 7.9 copy.85
  98.3 49.4 %all-gather.4.cloned.1.call-done = bf16[2560,1024]{1,0:T(8,128)(2,1)} async-done(((bf16[160,1024]{1,0:T(8,128)(2,1)}), bf16[2560,1024]{1,0:T(8,128)(2,1)}) %all-gather.4.cloned.1.call-update) | async-done | bytes 5242896 | tf_op jit(solution)/shard_map/all_gather | solution.py:122
  147.7 7.9 copy.84
  155.5 40.2 %while.26 = (s32[]{:T(128)}, f32[160,16,64]{0,2,1:T(8,128)}, f32[16,160]{1,0:T(8,128)S(1)}, bf16[2,1280,1024]{1,2,0:T(8,128)(2,1)}, s32[2,1280]{1,0:T(2,128)S(1)...) while((s32[]{:T(128)}, f32[160,16,64]{0,2,1:T(8,128)}, ...), condition=%wide.region_5.6_spmd.clone, body=%wide.region_3.5_spmd.clone.sunk | while | flops 859056768 | bytes 44253560 | solution.py:147
  155.5 4.4 constant_dynamic-slice_fusion.6
  160.1 6.5 fusion.124
  166.7 8.9 %fusion.125 = f32[160,16,64]{0,2,1:T(8,128)} fusion(bf16[1280,16,64]{0,2,1:T(8,128)(2,1)} %bitcast.209, f32[16,1280,160]{1,2,0:T(8,128)} %get-tuple-element.480, pred[160,1280]{1,0:T(8,128)(4,1)S(1)} %broadcast_compare_fusion.4, f32[160,16,64]{0,2,1:T(8,128)} %get-tuple-element.505, pred[]{:T(512)S(6)} %compare.6), kind=kOutput, calls=%fused_computation.10.clone.1 | convolution fusion | flops 429588480 | bytes 17244160 | tf_op jit(solution)/shard_map/while/body/eval_jaxpr/hqk,khd->qhd/dot_general | solution.py:139
  175.5 4.4 constant_dynamic-slice_fusion.6
  180.1 6.5 fusion.124
  186.7 9.1 %fusion.125 = f32[160,16,64]{0,2,1:T(8,128)} fusion(bf16[1280,16,64]{0,2,1:T(8,128)(2,1)} %bitcast.209, f32[16,1280,160]{1,2,0:T(8,128)} %get-tuple-element.480, pred[160,1280]{1,0:T(8,128)(4,1)S(1)} %broadcast_compare_fusion.4, f32[160,16,64]{0,2,1:T(8,128)} %get-tuple-element.505, pred[]{:T(512)S(6)} %compare.6), kind=kOutput, calls=%fused_computation.10.clone.1 | convolution fusion | flops 429588480 | bytes 17244160 | tf_op jit(solution)/shard_map/while/body/eval_jaxpr/hqk,khd->qhd/dot_general | solution.py:139
  195.8 2.9 multiply_reduce_fusion
  198.7 110.8 %while.27 = (s32[]{:T(128)}, f32[160,16,64]{0,2,1:T(8,128)}, bf16[2,1280,2048]{2,1,0:T(8,128)(2,1)}, bf16[2,1280,1024]{1,2,0:T(8,128)(2,1)}, s32[2,1280]{1,0:T(2...) while((s32[]{:T(128)}, f32[160,16,64]{0,2,1:T(8,128)}, ...), condition=%wide.region_9.10_spmd.clone, body=%wide.region_8.9_spmd.clone.sunk | while | flops 2137170048 | bytes 206425072 | solution.py:233
  198.9 4.4 constant_dynamic-slice_fusion.7
  203.2 6.6 fusion.136
  210.1 9.9 %fusion.137 = bf16[16,160,1280]{2,1,0:T(8,128)(2,1)S(1)} fusion(f32[16,1280,160]{1,2,0:T(8,128)} %fusion.136, bf16[1280,16,64]{0,2,1:T(8,128)(2,1)} %bitcast.211, bf16[160,16,64]{0,2,1:T(8,128)(2,1)} %get-tuple-element.555, f32[16,160]{1,0:T(8,128)S(1)} %bitcast.219, pred[160,1280]{1,0:T(8,128)(4,1)S(1)} %broadcast_compare_fusion.5), kind=kOutput, calls=%fused_computation.20.clone.1 | convolution fusion | flops 435814400 | bytes 22824960 | tf_op jit(solution)/shard_map/while/body/eval_jaxpr/qhd,khd->hqk/dot_general | solution.py:208
  221.1 2.3 copy-done.1
  223.4 3.8 copy-done.2
  227.1 3.7 fusion.139
  230.8 2.7 maximum_bitcast_fusion.2
  233.6 8.0 copy.108
  241.5 5.6 constant_dynamic-update-slice_fusion.2
  247.1 6.9 fusion.138
  254.0 4.4 constant_dynamic-slice_fusion.7
  258.4 6.6 fusion.136
  265.2 9.9 %fusion.137 = bf16[16,160,1280]{2,1,0:T(8,128)(2,1)S(1)} fusion(f32[16,1280,160]{1,2,0:T(8,128)} %fusion.136, bf16[1280,16,64]{0,2,1:T(8,128)(2,1)} %bitcast.211, bf16[160,16,64]{0,2,1:T(8,128)(2,1)} %get-tuple-element.555, f32[16,160]{1,0:T(8,128)S(1)} %bitcast.219, pred[160,1280]{1,0:T(8,128)(4,1)S(1)} %broadcast_compare_fusion.5), kind=kOutput, calls=%fused_computation.20.clone.1 | convolution fusion | flops 435814400 | bytes 22824960 | tf_op jit(solution)/shard_map/while/body/eval_jaxpr/qhd,khd->hqk/dot_general | solution.py:208
  276.3 2.3 copy-done.1
  278.5 3.8 copy-done.2
  282.3 3.7 fusion.139
  286.0 2.7 maximum_bitcast_fusion.2
  288.7 8.0 copy.108
  296.7 5.7 constant_dynamic-update-slice_fusion.2
  302.4 7.1 fusion.138
  310.4 3.1 convolution_convert_fusion.3
  317.7 3.5 multiply_subtract_fusion
  321.2 2.3 copy.93
  326.5 101.3 %reduce-scatter.8.cloned.1.call-done = bf16[160,2048]{1,0:T(8,128)(2,1)} async-done(((bf16[2560,2048]{1,0:T(8,128)(2,1)}), bf16[160,2048]{1,0:T(8,128)(2,1)}) %reduce-scatter.8.cloned.1.call-update) | async-done | bytes 655376 | tf_op jit(solution)/shard_map/reduce_scatter | solution.py:243
  434.0 2.3 reshape.294
  436.3 5.6 convolution_convert_fusion
  442.0 17.8 %all_gather.16 = bf16[320,1024]{1,0:T(8,128)(2,1)S(1)} all-gather(bf16[160,1024]{1,0:T(8,128)(2,1)S(1)} %copy-done.8), channel_id=1, replica_groups=mesh['dp'=16,'mlp'=2] {'mlp'}, dimensions={0}, use_global_device_ids=true | all-gather | bytes 983040 | tf_op jit(solution)/shard_map/all_gather | solution.py:160
  459.8 5.7 multiply_convert_fusion
  466.7 2.4 convolution_convert_fusion.5
  469.1 9.4 %all-gather = bf16[1,1,320,1024]{3,2,1,0:T(8,128)(2,1)S(1)} all-gather(bf16[1,1,160,1024]{3,2,1,0:T(8,128)(2,1)S(1)} %copy-done.11), channel_id=2, replica_groups=mesh['dp'=16,'mlp'=2] {'mlp'}, dimensions={2}, use_global_device_ids=true | all-gather | bytes 983040 | tf_op jit(solution)/shard_map/all_gather | solution.py:176
  478.5 6.4 fusion.68
  486.1 2.4 convolution_convert_fusion.4
  488.6 6.1 convolution_convert_fusion.2
  494.7 4.4 convolution_convert_fusion.1
  499.1 49.8 %reduce-scatter.12.cloned.1.call-done = bf16[1024,1536]{1,0:T(8,128)(2,1)} async-done(((bf16[1024,3072]{1,0:T(8,128)(2,1)}), bf16[1024,1536]{1,0:T(8,128)(2,1)}) %reduce-scatter.12.cloned.1.call-update) | async-done | bytes 3145744 | tf_op jit(solution)/shard_map/reduce_scatter | solution.py:266
  551.5 16.2 %reduce-scatter.6.cloned.1.call-done = bf16[160,1024]{1,0:T(8,128)(2,1)} async-done(((bf16[320,1024]{1,0:T(8,128)(2,1)}), bf16[160,1024]{1,0:T(8,128)(2,1)}) %reduce-scatter.6.cloned.1.call-update) | async-done | bytes 327696 | tf_op jit(solution)/shard_map/reduce_scatter | solution.py:164
  567.7 2.5 fusion.38
  570.4 15.7 %reduce-scatter.10.cloned.1.call-done = bf16[160,1024]{1,0:T(8,128)(2,1)} async-done(((bf16[320,1024]{1,0:T(8,128)(2,1)}), bf16[160,1024]{1,0:T(8,128)(2,1)}) %reduce-scatter.10.cloned.1.call-update) | async-done | bytes 327696 | tf_op jit(solution)/shard_map/reduce_scatter | solution.py:182
  586.1 6.1 fusion.53
  592.2 6.9 all-reduce.6
  599.4 63.3 %all-reduce.4 = (bf16[512]{0:T(512)(128)(2,1)S(1)}, bf16[512]{0:T(512)(128)(2,1)S(1)}, bf16[1536]{0:T(1024)(128)(2,1)S(1)}, bf16[512]{0:T(512)(128)(2,1)S(1)}, bf16[2048]{0:T(1024)(128)(2,1)S(1)}) all-reduce(bf16[512]{0:T(512)(128)(2,1)S(1)} %dynamic-slice.2, ...), channel_id=1, replica_groups=mesh['dp'=16,'mlp'=2] {'dp'}, use_global_device_ids=true, to_apply=%region_16.17 | all-reduce | flops 5120 | bytes 20480 | tf_op jit(solution)/shard_map/psum | solution.py:290
  665.0 2.2 fusion.52
  667.2 157.0 %all-reduce.9.cloned.1.call-done = (bf16[1024,1536]{1,0:T(8,128)(2,1)}, bf16[1024,512]{1,0:T(8,128)(2,1)}, bf16[1024,2048]{1,0:T(8,128)(2,1)}, bf16[2048,1024]{1,0:T(8,128)(2,1)}) async-done(((bf16[1024,1536]{1,0:T(8,128)(2,1)}, bf16[1024,512]{1,0:T(8,128)(2,1)}, bf16[1024,2048]{1,0:T(8,128)(2,1)}, bf16[2048,1024]{1,0:T(8,128)(2,1)}), (bf16[1024,1536]{1,0:T(8,128)(2,1)}, bf16[1024,512]{1,0:T(8,128)(2,1)}, ...) | async-done | bytes 12582928 | tf_op jit(solution)/shard_map/psum | solution.py:286
  824.2 6.8 convert_element_type.175
  831.0 4.4 convert_element_type.178
  835.5 3.6 convert_element_type.169
  (171 shorter events, 43.0 us)
Async XLA Ops:
  7.2 188.6 %copy-start = (bf16[1024,1024]{1,0:T(8,128)(2,1)S(1)}, bf16[1024,1024]{1,0:T(8,128)(2,1)}, u32[]{:S(2)}) copy-start(bf16[1024,1024]{1,0:T(8,128)(2,1)} %param.23) | copy-start | bytes 6291460
  7.2 83.2 %all-gather.6.cloned.1.call-start = ((), (), s32[]{:S(2)}) async-start(), calls=%async_computation.6 | async-start | bytes 5570560 | tf_op jit(solution)/shard_map/all_gather | solution.py:121
  10.2 15.1 %copy-start.17 = (f32[160,8]{1,0:T(8,128)}, f32[160,8]{1,0:T(8,128)S(1)}, u32[]{:S(2)}) copy-start(f32[160,8]{1,0:T(8,128)S(1)} %copy.82) | copy-start | bytes 15364
  12.0 1.2 copy-start.26
  13.3 0.6 copy-start.29
  15.1 4.1 copy-start.7
  19.2 1.5 copy-start.9
  23.5 1.7 copy-start.5
  31.8 115.8 %all-gather.4.cloned.1.call-start = ((), (), s32[]{:S(2)}) async-start(), calls=%async_computation.5 | async-start | bytes 5570560 | tf_op jit(solution)/shard_map/all_gather | solution.py:122
  33.8 4.3 copy-start.32
  33.8 394.0 %reduce-scatter.8.cloned.1.call-start = ((), (), s32[]{:S(2)}) async-start(), calls=%async_computation.8 | async-start | bytes 11141120 | tf_op jit(solution)/shard_map/reduce_scatter | solution.py:243
  155.5 40.2 %copy-start.10 = (bf16[1,1,160,1024]{3,2,1,0:T(8,128)(2,1)S(1)}, bf16[1,1,160,1024]{3,2,1,0:T(8,128)(2,1)}, u32[]{:S(2)}) copy-start(bf16[1,1,160,1024]{3,2,1,0:T(8,128)(2,1)} %param.29) | copy-start | bytes 983044
  203.2 6.6 copy-start.3
  220.0 3.3 copy-start.1
  220.1 7.1 copy-start.2
  258.4 6.6 copy-start.3
  275.2 3.3 copy-start.1
  275.2 7.1 copy-start.2
  309.5 1.0 copy-start.11
  309.5 5.7 copy-start.4
  309.5 189.6 %reduce-scatter.14.cloned.1.call-start = ((), (), s32[]{:S(2)}) async-start(), calls=%async_computation.11 | async-start | bytes 3145728 | tf_op jit(solution)/shard_map/reduce_scatter | solution.py:269
  313.5 4.2 copy-start.18
  313.5 235.4 %reduce-scatter.12.cloned.1.call-start = ((), (), s32[]{:S(2)}) async-start(), calls=%async_computation.10 | async-start | bytes 9437184 | tf_op jit(solution)/shard_map/reduce_scatter | solution.py:266
  317.7 6.9 copy-start.16
  431.0 0.9 copy-start.20
  432.5 3.8 copy-start.8
  432.5 3.8 copy-start.14
  441.9 17.9 %copy-start.35 = (f32[2048]{0:T(1024)S(1)}, f32[2048]{0:T(1024)}, u32[]{:S(2)}) copy-start(f32[2048]{0:T(1024)} %param.26) | copy-start | bytes 24580
  441.9 125.8 %reduce-scatter.6.cloned.1.call-start = ((), (), s32[]{:S(2)}) async-start(), calls=%async_computation.7 | async-start | bytes 983040 | tf_op jit(solution)/shard_map/reduce_scatter | solution.py:164
  459.8 5.7 copy-start.21
  459.8 6.8 copy-start.33
  465.6 1.1 copy-start.37
  469.1 117.0 %reduce-scatter.10.cloned.1.call-start = ((), (), s32[]{:S(2)}) async-start(), calls=%async_computation.9 | async-start | bytes 983040 | tf_op jit(solution)/shard_map/reduce_scatter | solution.py:182
  478.5 6.5 copy-start.22
  478.5 7.5 copy-start.34
  485.0 1.1 copy-start.39
  488.5 335.7 %all-reduce.9.cloned.1.call-start = ((), (), s32[]{:S(2)}) async-start(), calls=%async_computation.12 | async-start | bytes 25165824 | tf_op jit(solution)/shard_map/psum | solution.py:286
  488.6 6.1 copy-start.23
  488.6 6.1 copy-start.38
  548.9 0.7 copy-start.36
  548.9 18.8 %copy-start.6 = (bf16[1,1,160,1024]{3,2,1,0:T(8,128)(2,1)S(1)}, bf16[1,1,160,1024]{3,2,1,0:T(8,128)(2,1)}, u32[]{:S(2)}) copy-start(bf16[1,1,160,1024]{3,2,1,0:T(8,128)(2,1)} %param.17) | copy-start | bytes 983044
  548.9 18.8 %copy-start.24 = (f32[1024]{0:T(1024)S(1)}, f32[1024]{0:T(1024)}, u32[]{:S(2)}) copy-start(f32[1024]{0:T(1024)} %param.28) | copy-start | bytes 12292
  548.9 18.8 %copy-start.25 = (f32[1024]{0:T(1024)S(1)}, f32[1024]{0:T(1024)}, u32[]{:S(2)}) copy-start(f32[1024]{0:T(1024)} %param.24) | copy-start | bytes 12292
  549.0 37.1 %copy-start.27 = (f32[160]{0:T(256)S(1)}, f32[160]{0:T(256)}, u32[]{:S(2)}) copy-start(f32[160]{0:T(256)} %copy-done.26) | copy-start | bytes 1924
  549.0 37.1 %copy-start.28 = (f32[1024]{0:T(1024)S(1)}, f32[1024]{0:T(1024)}, u32[]{:S(2)}) copy-start(f32[1024]{0:T(1024)} %param.19) | copy-start | bytes 12292
  549.0 37.1 %copy-start.30 = (f32[160]{0:T(256)S(1)}, f32[160]{0:T(256)}, u32[]{:S(2)}) copy-start(f32[160]{0:T(256)} %copy-done.29) | copy-start | bytes 1924
  567.7 2.5 copy-start.15
  663.9 176.8 %copy-start.31 = (f32[512]{0:T(512)}, f32[512]{0:T(512)S(1)}, u32[]{:S(2)}) copy-start(f32[512]{0:T(512)S(1)} %convert_element_type.173) | copy-start | bytes 6148
  824.2 6.8 copy-start.12
  831.0 4.4 copy-start.13
  835.5 3.6 copy-start.19
Sparse Core Ops, SparseCore 0:
  31.9 58.4 all-gather.5
  93.3 54.3 all-gather.3
  309.6 118.0 reduce-scatter.7
  430.4 38.5 reduce-scatter.13
  471.8 77.1 reduce-scatter.11
  551.6 16.0 reduce-scatter.5
  570.0 16.0 reduce-scatter.9
  591.2 232.9 all-reduce.8
where the time goes:
time: 855 us; the launch traced here: 849 us
  waiting for transfers between devices  442 us (52%)
  matrix products  139 us (16%)
  local copies, waits for them, and re-layouts  107 us (13%)
  blocking collectives  97.4 us (11%)
  other arithmetic  44.8 us (5%)
  between operations  17 us (2%)
    psum x1, waiting for transfers between devices, local(): lax.psum(part_qkv.astype(jnp.bfloat16), 'dp').astype(jnp.float32)  157 us
    reduce_scatter x1, waiting for transfers between devices, local(): lax.psum_scatter(grad_kv_sum.astype(jnp.bfloat16), 'dp', scatter_dimensio...  101 us
    psum x1, blocking collectives, local(): lax.psum(part_gain.astype(jnp.bfloat16), 'dp').astype(jnp.float32)  63.3 us
    all_gather x1, waiting for transfers between devices, local(): keys_piece = lax.all_gather(keys_flat, 'dp', axis=0, tiled=True)  52.1 us
    reduce_scatter x1, waiting for transfers between devices, local(): lax.psum_scatter(grad_w_qkv.astype(jnp.bfloat16), 'mlp', scatter_dimensio...  49.8 us
    all_gather x1, waiting for transfers between devices, local(): values_piece = lax.all_gather(values_flat, 'dp', axis=0, tiled=True)  49.4 us
    dynamic_update_slice x4, local copies, waits for them, and re-layouts, local(): lax.scan(back_one_block, grad_query_sum, (keys_piece.reshape(blocks, back...  27.2 us
    unnamed x83, local copies, waits for them, and re-layouts  23 us
  transfers between devices with their start and end apart: 8, of which 7 were waited for; matrix products, arithmetic and copies ran while one was open for 10% of the time, Pallas kernels for 0%

commit v1 on v0

--- a/solution.py
+++ b/solution.py
@@ -11,6 +11,27 @@
 ROPE_BASE = 10000.0
 SQRT_HALF = 1.0 / math.sqrt(2.0)
 INV_ROOT_TWO_PI = 1.0 / math.sqrt(2.0 * math.pi)
+
+
+def laid_out(parts, dim):
+    parts = jnp.moveaxis(parts, 0, dim)
+    dims = parts.shape
+    return parts.reshape(*dims[:dim], dims[dim] * dims[dim + 1], *dims[dim + 2 :])
+
+
+def doubled(shard, axis):
+    length, index = (lax.axis_size(axis), lax.axis_index(axis))
+    blocks, bit = (shard[None], 1)
+    while bit < length:
+        other = lax.ppermute(blocks, axis, [(i, i ^ bit) for i in range(length)])
+        low = index & bit == 0
+        blocks = jnp.concatenate([jnp.where(low, blocks, other), jnp.where(low, other, blocks)])
+        bit *= 2
+    return blocks
+
+
+def doubled_up(value, axis, dim):
+    return laid_out(doubled(value, axis), dim)
 
 
 def rotate(values, positions, sign_factor):
@@ -118,7 +139,7 @@
         jnp.zeros((tok_count, HEADS, HEAD_DIM), jnp.float32),
         jnp.zeros((HEADS, tok_count), jnp.float32),
     )
-    keys_piece = lax.all_gather(keys_flat, "dp", axis=0, tiled=True)
+    keys_piece = doubled_up(keys_flat, "dp", 0)
     values_piece = lax.all_gather(values_flat, "dp", axis=0, tiled=True)
     piece_rows = keys_piece.shape[0]
     blocks = piece_count(piece_rows)

time: 855 us -> 998 us (1.17)
  waiting for transfers between devices: 442 us -> 542 us
  matrix products: 139 us -> 155 us
  other arithmetic: 44.8 us -> 56.1 us
    ppermute x0 -> x4, waiting for transfers between devices: none -> 200 us  [doubled(): other = lax.ppermute(blocks, axis, [(i, i ^ bit) for i in range(length)])]
    all_gather x1, waiting for transfers between devices: 52.1 us -> 0.02 us  [local(): keys_piece = lax.all_gather(keys_flat, 'dp', axis=0, tiled=True)]
    all_gather x1, waiting for transfers between devices: 49.4 us -> 0.01 us  [local(): values_piece = lax.all_gather(values_flat, 'dp', axis=0, tiled=True)]
    dynamic_slice x8 -> x16, local copies, waits for them, and re-layouts: 17.6 us -> 38.8 us  [local(): lax.scan(attend_one_block, start_state, (keys_piece.reshape(blocks, sub_r...]
    unnamed x83 -> x92, local copies, waits for them, and re-layouts: 23 us -> 19.4 us
  transfers between devices with their start and end apart: 8 -> 12, of which waited for: 7 -> 9; matrix products, arithmetic and copies ran while one was open for 10% -> 17% of each run, Pallas kernels for 0% -> 0%
where the time goes in v1:
time: 998 us; the launch traced here: 991 us
  waiting for transfers between devices  542 us (54%)
  matrix products  155 us (16%)
  local copies, waits for them, and re-layouts  115 us (12%)
  blocking collectives  97.3 us (10%)
  other arithmetic  56.1 us (6%)
  between operations  16.9 us (2%)
    ppermute x4, waiting for transfers between devices, doubled(): other = lax.ppermute(blocks, axis, [(i, i ^ bit) for i in range(length)])  200 us
    psum x1, waiting for transfers between devices, local(): lax.psum(part_qkv.astype(jnp.bfloat16), 'dp').astype(jnp.float32)  157 us
    reduce_scatter x1, waiting for transfers between devices, local(): lax.psum_scatter(grad_kv_sum.astype(jnp.bfloat16), 'dp', scatter_dimensio...  103 us
    psum x1, blocking collectives, local(): lax.psum(part_gain.astype(jnp.bfloat16), 'dp').astype(jnp.float32)  63.2 us
    reduce_scatter x1, waiting for transfers between devices, local(): lax.psum_scatter(grad_w_qkv.astype(jnp.bfloat16), 'mlp', scatter_dimensio...  49.9 us
    dynamic_slice x16, local copies, waits for them, and re-layouts, local(): lax.scan(attend_one_block, start_state, (keys_piece.reshape(blocks, sub_r...  38.8 us
    dynamic_update_slice x4, local copies, waits for them, and re-layouts, local(): lax.scan(back_one_block, grad_query_sum, (keys_piece.reshape(blocks, back...  27.4 us
  transfers between devices with their start and end apart: 12, of which 9 were waited for; matrix products, arithmetic and copies ran while one was open for 17% of the time, Pallas kernels for 0%

profile of v1, /device:TPU:0, one launch (start us, length us, event | category | flops | bytes accessed | tf_op | source)
XLA Modules:
  0.0 990.8 jit_solution(10866736295139719446)
XLA Ops:
  11.6 4.1 convolution_add_fusion
  20.7 2.5 fusion.66
  30.0 2.9 collective-permute-start.1
  32.9 16.0 %collective-permute-done.1 = bf16[2,160,1024]{2,1,0:T(8,128)(2,1)} collective-permute-done((bf16[2,160,1024]{2,1,0:T(8,128)(2,1)S(1)}, bf16[2,160,1024]{2,1,0:T(8,128)(2,1)}, u32[]{:S(2)}, u32[]{:S(2)}) %collective-permute-start.1) | collective-permute-done | bytes 655392 | tf_op jit(solution)/shard_map/ppermute | solution.py:26
  53.9 46.0 %collective-permute-done.2 = bf16[4,160,1024]{2,1,0:T(8,128)(2,1)} collective-permute-done((bf16[4,160,1024]{2,1,0:T(8,128)(2,1)}, bf16[4,160,1024]{2,1,0:T(8,128)(2,1)}, u32[]{:S(2)}, u32[]{:S(2)}) %collective-permute-start.2) | collective-permute-done | bytes 1310752 | tf_op jit(solution)/shard_map/ppermute | solution.py:26
  103.9 2.4 collective-permute-start.3
  112.3 2.4 copy.86
  114.9 136.5 %collective-permute-done.3 = bf16[8,160,1024]{2,1,0:T(8,128)(2,1)} collective-permute-done((bf16[8,160,1024]{2,1,0:T(8,128)(2,1)}, bf16[8,160,1024]{2,1,0:T(8,128)(2,1)}, u32[]{:S(2)}, u32[]{:S(2)}) %collective-permute-start.3) | collective-permute-done | bytes 2621472 | tf_op jit(solution)/shard_map/ppermute | solution.py:26
  251.4 2.3 broadcast_select_fusion.1
  253.7 2.8 pad_maximum_fusion
  256.5 7.9 copy.84
  264.4 59.1 %while.26 = (s32[]{:T(128)}, f32[160,16,64]{0,2,1:T(8,128)}, f32[16,160]{1,0:T(8,128)S(1)}, bf16[2,1280,1024]{1,2,0:T(8,128)(2,1)}, s32[2,1280]{1,0:T(2,128)S(1)...) while((s32[]{:T(128)}, f32[160,16,64]{0,2,1:T(8,128)}, ...), condition=%wide.region_5.6_spmd.clone, body=%wide.region_3.5_spmd.clone.sunk | while | flops 859056768 | bytes 65225132 | solution.py:168
  265.3 3.5 constant_dynamic-slice_fusion.9
  268.8 4.5 copy.112
  273.3 10.0 %fusion.124 = (f32[16,160]{1,0:T(8,128)S(1)}, f32[16,1280,160]{1,2,0:T(8,128)}) fusion(pred[160,1280]{1,0:T(8,128)(4,1)} %broadcast_compare_fusion.4, bf16[1280,16,64]{0,2,1:T(8,128)(2,1)} %bitcast.214, bf16[160,16,64]{0,2,1:T(8,128)(2,1)} %get-tuple-element.514), kind=kOutput, calls=%fused_computation.3.clone.1 | convolution fusion | flops 429258240 | bytes 16271360 | tf_op jit(solution)/shard_map/while/body/eval_jaxpr/qhd,khd->hqk/dot_general | solution.py:154
  285.0 8.8 fusion.125
  294.7 3.5 constant_dynamic-slice_fusion.9
  298.2 4.5 copy.112
  302.7 10.0 %fusion.124 = (f32[16,160]{1,0:T(8,128)S(1)}, f32[16,1280,160]{1,2,0:T(8,128)}) fusion(pred[160,1280]{1,0:T(8,128)(4,1)} %broadcast_compare_fusion.4, bf16[1280,16,64]{0,2,1:T(8,128)(2,1)} %bitcast.214, bf16[160,16,64]{0,2,1:T(8,128)(2,1)} %get-tuple-element.514), kind=kOutput, calls=%fused_computation.3.clone.1 | convolution fusion | flops 429258240 | bytes 16271360 | tf_op jit(solution)/shard_map/while/body/eval_jaxpr/qhd,khd->hqk/dot_general | solution.py:154
  314.4 9.1 fusion.125
  323.5 2.9 multiply_reduce_fusion
  326.4 124.0 %while.27 = (s32[]{:T(128)}, f32[160,16,64]{0,2,1:T(8,128)}, bf16[2,1280,2048]{2,1,0:T(8,128)(2,1)}, bf16[2,1280,1024]{2,1,0:T(8,128)(2,1)}, s32[2,1280]{1,0:T(2...) while((s32[]{:T(128)}, f32[160,16,64]{0,2,1:T(8,128)}, ...), condition=%wide.region_9.10_spmd.clone, body=%wide.region_8.9_spmd.clone.sunk | while | flops 2137170048 | bytes 172346448 | solution.py:254
  326.7 3.5 constant_dynamic-slice_fusion.10
  330.1 4.5 copy.113
  334.7 8.6 fusion.136
  345.2 10.0 %fusion.137 = bf16[16,160,1280]{2,1,0:T(8,128)(2,1)S(1)} fusion(f32[16,1280,160]{1,2,0:T(8,128)} %fusion.136, bf16[1280,16,64]{0,2,1:T(8,128)(2,1)} %bitcast.216, bf16[160,16,64]{0,2,1:T(8,128)(2,1)} %get-tuple-element.549, f32[16,160]{1,0:T(8,128)S(1)} %bitcast.225, pred[160,1280]{1,0:T(8,128)(4,1)S(1)} %broadcast_compare_fusion.5), kind=kOutput, calls=%fused_computation.20.clone.1 | convolution fusion | flops 435814400 | bytes 22824960 | tf_op jit(solution)/shard_map/while/body/eval_jaxpr/qhd,khd->hqk/dot_general | solution.py:229
  358.0 7.2 fusion.139
  365.2 2.7 maximum_bitcast_fusion.2
  367.9 8.0 copy.114
  375.9 5.7 constant_dynamic-update-slice_fusion.2
  381.6 6.0 fusion.138
  388.5 3.5 constant_dynamic-slice_fusion.10
  392.0 4.5 copy.113
  396.5 8.6 fusion.136
  407.1 10.0 %fusion.137 = bf16[16,160,1280]{2,1,0:T(8,128)(2,1)S(1)} fusion(f32[16,1280,160]{1,2,0:T(8,128)} %fusion.136, bf16[1280,16,64]{0,2,1:T(8,128)(2,1)} %bitcast.216, bf16[160,16,64]{0,2,1:T(8,128)(2,1)} %get-tuple-element.549, f32[16,160]{1,0:T(8,128)S(1)} %bitcast.225, pred[160,1280]{1,0:T(8,128)(4,1)S(1)} %broadcast_compare_fusion.5), kind=kOutput, calls=%fused_computation.20.clone.1 | convolution fusion | flops 435814400 | bytes 22824960 | tf_op jit(solution)/shard_map/while/body/eval_jaxpr/qhd,khd->hqk/dot_general | solution.py:229
  419.9 7.2 fusion.139
  427.1 2.7 maximum_bitcast_fusion.2
  429.8 8.0 copy.114
  437.7 5.7 constant_dynamic-update-slice_fusion.2
  443.5 6.0 fusion.138
  451.4 3.1 convolution_convert_fusion.3
  458.4 3.5 multiply_subtract_fusion
  467.2 103.1 %reduce-scatter.8.cloned.1.call-done = bf16[160,2048]{1,0:T(8,128)(2,1)} async-done(((bf16[2560,2048]{1,0:T(8,128)(2,1)}), bf16[160,2048]{1,0:T(8,128)(2,1)}) %reduce-scatter.8.cloned.1.call-update) | async-done | bytes 655376 | tf_op jit(solution)/shard_map/reduce_scatter | solution.py:264
  576.5 2.3 reshape.304
  578.8 5.6 convolution_convert_fusion
  584.5 17.8 %all_gather.14 = bf16[320,1024]{1,0:T(8,128)(2,1)S(1)} all-gather(bf16[160,1024]{1,0:T(8,128)(2,1)S(1)} %copy-done.12), channel_id=1, replica_groups=mesh['dp'=16,'mlp'=2] {'mlp'}, dimensions={0}, use_global_device_ids=true | all-gather | bytes 983040 | tf_op jit(solution)/shard_map/all_gather | solution.py:181
  602.3 5.7 multiply_convert_fusion
  609.1 2.4 convolution_convert_fusion.5
  611.6 9.3 all-gather
  620.9 6.5 fusion.68
  628.5 2.4 convolution_convert_fusion.4
  631.0 6.1 convolution_convert_fusion.2
  637.1 4.4 convolution_convert_fusion.1
  641.5 49.9 %reduce-scatter.12.cloned.1.call-done = bf16[1024,1536]{1,0:T(8,128)(2,1)} async-done(((bf16[1024,3072]{1,0:T(8,128)(2,1)}), bf16[1024,1536]{1,0:T(8,128)(2,1)}) %reduce-scatter.12.cloned.1.call-update) | async-done | bytes 3145744 | tf_op jit(solution)/shard_map/reduce_scatter | solution.py:287
  694.0 16.2 %reduce-scatter.6.cloned.1.call-done = bf16[160,1024]{1,0:T(8,128)(2,1)} async-done(((bf16[320,1024]{1,0:T(8,128)(2,1)}), bf16[160,1024]{1,0:T(8,128)(2,1)}) %reduce-scatter.6.cloned.1.call-update) | async-done | bytes 327696 | tf_op jit(solution)/shard_map/reduce_scatter | solution.py:185
  710.2 2.5 fusion.38
  712.9 15.7 %reduce-scatter.10.cloned.1.call-done = bf16[160,1024]{1,0:T(8,128)(2,1)} async-done(((bf16[320,1024]{1,0:T(8,128)(2,1)}), bf16[160,1024]{1,0:T(8,128)(2,1)}) %reduce-scatter.10.cloned.1.call-update) | async-done | bytes 327696 | tf_op jit(solution)/shard_map/reduce_scatter | solution.py:203
  728.6 6.1 fusion.53
  734.6 6.9 all-reduce.6
  741.9 63.2 %all-reduce.4 = (bf16[512]{0:T(512)(128)(2,1)S(1)}, bf16[512]{0:T(512)(128)(2,1)S(1)}, bf16[1536]{0:T(1024)(128)(2,1)S(1)}, bf16[512]{0:T(512)(128)(2,1)S(1)}, bf16[2048]{0:T(1024)(128)(2,1)S(1)}) all-reduce(bf16[512]{0:T(512)(128)(2,1)S(1)} %dynamic-slice.2, ...), channel_id=1, replica_groups=mesh['dp'=16,'mlp'=2] {'dp'}, use_global_device_ids=true, to_apply=%region_16.17 | all-reduce | flops 5120 | bytes 20480 | tf_op jit(solution)/shard_map/psum | solution.py:311
  809.7 157.1 %all-reduce.9.cloned.1.call-done = (bf16[1024,1536]{1,0:T(8,128)(2,1)}, bf16[1024,512]{1,0:T(8,128)(2,1)}, bf16[1024,2048]{1,0:T(8,128)(2,1)}, bf16[2048,1024]{1,0:T(8,128)(2,1)}) async-done(((bf16[1024,1536]{1,0:T(8,128)(2,1)}, bf16[1024,512]{1,0:T(8,128)(2,1)}, bf16[1024,2048]{1,0:T(8,128)(2,1)}, bf16[2048,1024]{1,0:T(8,128)(2,1)}), (bf16[1024,1536]{1,0:T(8,128)(2,1)}, bf16[1024,512]{1,0:T(8,128)(2,1)}, ...) | async-done | bytes 12582928 | tf_op jit(solution)/shard_map/psum | solution.py:307
  966.7 6.8 convert_element_type.189
  973.5 4.4 convert_element_type.192
  978.0 3.6 convert_element_type.183
  (234 shorter events, 74.0 us)
Async XLA Ops:
  7.2 316.3 %copy-start = (bf16[1024,1024]{1,0:T(8,128)(2,1)S(1)}, bf16[1024,1024]{1,0:T(8,128)(2,1)}, u32[]{:S(2)}) copy-start(bf16[1024,1024]{1,0:T(8,128)(2,1)} %param.23) | copy-start | bytes 6291460
  7.2 249.3 %all-gather.4.cloned.1.call-start = ((), (), s32[]{:S(2)}) async-start(), calls=%async_computation.5 | async-start | bytes 5570560 | tf_op jit(solution)/shard_map/all_gather | solution.py:143
  8.5 1.2 copy-start.33
  11.6 4.1 copy-start.11
  11.6 6.3 copy-start.39
  15.7 1.3 copy-start.13
  17.8 308.7 %all-gather.6.cloned.1.call-start = ((), (), s32[]{:S(2)}) async-start(), calls=%async_computation.7 | async-start | bytes 5570560 | tf_op jit(solution)/shard_map/all_gather | solution.py:212
  19.9 89.5 %copy-start.23 = (f32[160,8]{1,0:T(8,128)}, f32[160,8]{1,0:T(8,128)S(1)}, u32[]{:S(2)}) copy-start(f32[160,8]{1,0:T(8,128)S(1)} %copy.82) | copy-start | bytes 15364
  27.3 1.8 collective-permute-start
  30.0 19.0 %collective-permute-start.1 = (bf16[2,160,1024]{2,1,0:T(8,128)(2,1)S(1)}, bf16[2,160,1024]{2,1,0:T(8,128)(2,1)}, u32[]{:S(2)}, u32[]{:S(2)}) collective-permute-start(bf16[2,160,1024]{2,1,0:T(8,128)(2,1)S(1)} %pad_maximum_fusion.4), channel_id=1, source_target_pairs={{0,4},{2,6},{4,0},{6,2},{8,12},{10,14},{12,8},{14,10},{16,20},{18,... | collective-permute-start | bytes 1966088 | tf_op jit(solution)/shard_map/ppermute | solution.py:26
  52.4 47.5 %collective-permute-start.2 = (bf16[4,160,1024]{2,1,0:T(8,128)(2,1)}, bf16[4,160,1024]{2,1,0:T(8,128)(2,1)}, u32[]{:S(2)}, u32[]{:S(2)}) collective-permute-start(bf16[4,160,1024]{2,1,0:T(8,128)(2,1)} %pad_maximum_fusion.2), channel_id=1, source_target_pairs={{0,8},{2,10},{4,12},{6,14},{8,0},{10,2},{12,4},{14,6},{16,24},{18,... | collective-permute-start | bytes 3932168 | tf_op jit(solution)/shard_map/ppermute | solution.py:26
  101.5 1.9 copy-start.7
  101.5 2.3 copy-start.9
  103.9 147.6 %collective-permute-start.3 = (bf16[8,160,1024]{2,1,0:T(8,128)(2,1)}, bf16[8,160,1024]{2,1,0:T(8,128)(2,1)}, u32[]{:S(2)}, u32[]{:S(2)}) collective-permute-start(bf16[8,160,1024]{2,1,0:T(8,128)(2,1)} %pad_maximum_fusion.1), channel_id=1, source_target_pairs={{0,16},{2,18},{4,20},{6,22},{8,24},{10,26},{12,28},{14,30},{16,0},... | collective-permute-start | bytes 7864328 | tf_op jit(solution)/shard_map/ppermute | solution.py:26
  107.5 462.8 %reduce-scatter.8.cloned.1.call-start = ((), (), s32[]{:S(2)}) async-start(), calls=%async_computation.8 | async-start | bytes 11141120 | tf_op jit(solution)/shard_map/reduce_scatter | solution.py:264
  110.9 140.6 %copy-start.8 = (bf16[4,160,1024]{2,1,0:T(8,128)(2,1)S(1)}, bf16[4,160,1024]{2,1,0:T(8,128)(2,1)}, u32[]{:S(2)}) copy-start(bf16[4,160,1024]{2,1,0:T(8,128)(2,1)} %copy-done.7) | copy-start | bytes 3932164
  264.4 59.1 %copy-start.15 = (bf16[1,1,160,1024]{3,2,1,0:T(8,128)(2,1)S(1)}, bf16[1,1,160,1024]{3,2,1,0:T(8,128)(2,1)}, u32[]{:S(2)}) copy-start(bf16[1,1,160,1024]{3,2,1,0:T(8,128)(2,1)} %param.29) | copy-start | bytes 983044
  268.8 14.5 %slice-start = ((s8[5242880]{0:T(1024)(128)(4,1)}), s8[1048576]{0:T(1024)(128)(4,1)S(1)}, s32[]{:S(2)}) async-start(s8[5242880]{0:T(1024)(128)(4,1)} %bitcast.210), calls=%async_computation.13 | async-start | bytes 2097152 | tf_op jit(solution)/shard_map/while
  273.3 10.0 %slice-start.1 = ((s8[5242880]{0:T(1024)(128)(4,1)}), s8[4194304]{0:T(1024)(128)(4,1)S(1)}, s32[]{:S(2)}) async-start(s8[5242880]{0:T(1024)(128)(4,1)} %bitcast.210), calls=%async_computation.14 | async-start | bytes 8388608 | tf_op jit(solution)/shard_map/while
  298.2 14.5 %slice-start = ((s8[5242880]{0:T(1024)(128)(4,1)}), s8[1048576]{0:T(1024)(128)(4,1)S(1)}, s32[]{:S(2)}) async-start(s8[5242880]{0:T(1024)(128)(4,1)} %bitcast.210), calls=%async_computation.13 | async-start | bytes 2097152 | tf_op jit(solution)/shard_map/while
  302.7 10.0 %slice-start.1 = ((s8[5242880]{0:T(1024)(128)(4,1)}), s8[4194304]{0:T(1024)(128)(4,1)S(1)}, s32[]{:S(2)}) async-start(s8[5242880]{0:T(1024)(128)(4,1)} %bitcast.210), calls=%async_computation.14 | async-start | bytes 8388608 | tf_op jit(solution)/shard_map/while
  330.1 13.4 %slice-start.2 = ((s8[5242880]{0:T(1024)(128)(4,1)}), s8[1048576]{0:T(1024)(128)(4,1)S(1)}, s32[]{:S(2)}) async-start(s8[5242880]{0:T(1024)(128)(4,1)} %bitcast.212), calls=%async_computation.15 | async-start | bytes 2097152 | tf_op jit(solution)/shard_map/while
  334.7 8.8 slice-start.3
  345.2 10.0 %copy-start.2 = (bf16[160,16,64]{0,2,1:T(8,128)(2,1)S(1)}, bf16[160,16,64]{0,2,1:T(8,128)(2,1)}, u32[]{:S(2)}) copy-start(bf16[160,16,64]{0,2,1:T(8,128)(2,1)} %get-tuple-element.547) | copy-start | bytes 983044 | tf_op jit(solution)/shard_map/while
  355.2 2.8 copy-start.1
  355.2 2.8 copy-start.6
  375.9 5.7 copy-start.3
  387.6 1.0 copy-start.4
  392.0 13.4 %slice-start.2 = ((s8[5242880]{0:T(1024)(128)(4,1)}), s8[1048576]{0:T(1024)(128)(4,1)S(1)}, s32[]{:S(2)}) async-start(s8[5242880]{0:T(1024)(128)(4,1)} %bitcast.212), calls=%async_computation.15 | async-start | bytes 2097152 | tf_op jit(solution)/shard_map/while
  396.5 8.8 slice-start.3
  407.1 10.0 %copy-start.2 = (bf16[160,16,64]{0,2,1:T(8,128)(2,1)S(1)}, bf16[160,16,64]{0,2,1:T(8,128)(2,1)}, u32[]{:S(2)}) copy-start(bf16[160,16,64]{0,2,1:T(8,128)(2,1)} %get-tuple-element.547) | copy-start | bytes 983044 | tf_op jit(solution)/shard_map/while
  417.1 2.8 copy-start.1
  417.1 2.8 copy-start.6
  437.7 5.7 copy-start.3
  450.4 5.5 copy-start.5
  450.4 191.1 %reduce-scatter.14.cloned.1.call-start = ((), (), s32[]{:S(2)}) async-start(), calls=%async_computation.11 | async-start | bytes 3145728 | tf_op jit(solution)/shard_map/reduce_scatter | solution.py:290
  454.4 4.0 copy-start.24
  454.5 237.0 %reduce-scatter.12.cloned.1.call-start = ((), (), s32[]{:S(2)}) async-start(), calls=%async_computation.10 | async-start | bytes 9437184 | tf_op jit(solution)/shard_map/reduce_scatter | solution.py:287
  458.4 6.9 copy-start.25
  575.1 3.8 copy-start.12
  575.1 3.8 copy-start.19
  584.4 17.9 %copy-start.42 = (f32[2048]{0:T(1024)S(1)}, f32[2048]{0:T(1024)}, u32[]{:S(2)}) copy-start(f32[2048]{0:T(1024)} %param.26) | copy-start | bytes 24580
  584.4 125.8 %reduce-scatter.6.cloned.1.call-start = ((), (), s32[]{:S(2)}) async-start(), calls=%async_computation.6 | async-start | bytes 983040 | tf_op jit(solution)/shard_map/reduce_scatter | solution.py:185
  602.3 5.7 copy-start.28
  602.3 6.8 copy-start.40
  608.1 1.1 copy-start.44
  611.5 117.0 %reduce-scatter.10.cloned.1.call-start = ((), (), s32[]{:S(2)}) async-start(), calls=%async_computation.9 | async-start | bytes 983040 | tf_op jit(solution)/shard_map/reduce_scatter | solution.py:203
  620.9 6.5 copy-start.29
  620.9 7.6 copy-start.41
  627.4 1.1 copy-start.46
  630.9 335.8 %all-reduce.9.cloned.1.call-start = ((), (), s32[]{:S(2)}) async-start(), calls=%async_computation.12 | async-start | bytes 25165824 | tf_op jit(solution)/shard_map/psum | solution.py:307
  631.0 6.1 copy-start.30
  631.0 6.1 copy-start.45
  691.4 18.8 %copy-start.10 = (bf16[1,1,160,1024]{3,2,1,0:T(8,128)(2,1)S(1)}, bf16[1,1,160,1024]{3,2,1,0:T(8,128)(2,1)}, u32[]{:S(2)}) copy-start(bf16[1,1,160,1024]{3,2,1,0:T(8,128)(2,1)} %param.17) | copy-start | bytes 983044
  691.4 18.8 %copy-start.31 = (f32[1024]{0:T(1024)S(1)}, f32[1024]{0:T(1024)}, u32[]{:S(2)}) copy-start(f32[1024]{0:T(1024)} %param.28) | copy-start | bytes 12292
  691.4 18.8 %copy-start.32 = (f32[1024]{0:T(1024)S(1)}, f32[1024]{0:T(1024)}, u32[]{:S(2)}) copy-start(f32[1024]{0:T(1024)} %param.24) | copy-start | bytes 12292
  691.5 37.1 %copy-start.34 = (f32[160]{0:T(256)S(1)}, f32[160]{0:T(256)}, u32[]{:S(2)}) copy-start(f32[160]{0:T(256)} %copy-done.33) | copy-start | bytes 1924
  691.5 37.1 %copy-start.35 = (f32[1024]{0:T(1024)S(1)}, f32[1024]{0:T(1024)}, u32[]{:S(2)}) copy-start(f32[1024]{0:T(1024)} %param.19) | copy-start | bytes 12292
  691.5 37.1 %copy-start.37 = (f32[160]{0:T(256)S(1)}, f32[160]{0:T(256)}, u32[]{:S(2)}) copy-start(f32[160]{0:T(256)} %copy-done.36) | copy-start | bytes 1924
  710.2 2.5 copy-start.20
  806.3 176.9 %copy-start.38 = (f32[512]{0:T(512)}, f32[512]{0:T(512)S(1)}, u32[]{:S(2)}) copy-start(f32[512]{0:T(512)S(1)} %convert_element_type.187) | copy-start | bytes 6148
  966.7 6.8 copy-start.17
  973.5 4.4 copy-start.18
  978.0 3.6 copy-start.26
  (8 other events, 6.4 us)
Sparse Core Ops, SparseCore 0:
  17.9 66.8 all-gather.3
  107.6 114.6 all-gather.5
  450.6 119.6 reduce-scatter.7
  573.0 38.5 reduce-scatter.13
  614.3 77.1 reduce-scatter.11
  694.1 16.0 reduce-scatter.5
  712.5 16.0 reduce-scatter.9
  733.7 232.9 all-reduce.8
